TPU v7x, 32 devices: a whole 2x2x4 slice. The times are simulated.
32 devices in a mesh: seq: 16 (over z, y, core), res: 2 (over x).
Axes of the slice: x: 2, y: 2, z: 4, core: 2. Of those that a mesh axis runs over, the one named last changes fastest.
Arguments:
- homolog_embedding: bfloat16 [256, 128, 256], P('seq', 'res'), may hold values from -6 to 6
- pair_features: bfloat16 [128, 128, 128], P('seq', 'res'), may hold values from -6 to 6
- row_present_mask: int32 [256], replicated, may hold values 0 or 1
- residue_keep_mask: int32 [128], replicated, may hold values 0 or 1
- query_weight: bfloat16 [256, 256], replicated, may hold values from -64 to 64
- key_weight: bfloat16 [256, 256], replicated, may hold values from -1 to 1
- content_matrix: bfloat16 [256, 256], replicated, may hold values from -0.375 to 0.375
- sigmoid_switch_matrix: bfloat16 [256, 256], replicated, may hold values from -0.375 to 0.375
- focus_merge_matrix: bfloat16 [256, 256], replicated, may hold values from -0.375 to 0.375
- widening_matrix: bfloat16 [256, 1024], replicated, may hold values from -0.375 to 0.375
- narrowing_matrix: bfloat16 [1024, 256], replicated, may hold values from -0.1875 to 0.1875
- first_factor_matrix: bfloat16 [256, 32], replicated, may hold values from -0.375 to 0.375
- second_factor_matrix: bfloat16 [256, 32], replicated, may hold values from -0.375 to 0.375
- outer_product_weight: bfloat16 [1024, 128], replicated, may hold values from -1 to 1
- outer_product_bias: float32 [128], replicated, may hold values from -3 to 3
- pair_up_weight: bfloat16 [128, 512], replicated, may hold values from -0.5 to 0.5
- pair_down_weight: bfloat16 [512, 128], replicated, may hold values from -0.25 to 0.25
Outputs:
- msa_update: bfloat16 [256, 128, 256], P('seq', 'res')
- pair_update: bfloat16 [128, 128, 128], P('seq', 'res')
All inputs are finite; a program needn't handle non-finite values.
Results may differ from a plain program's by a relative error of at most 0.012.
Values may be sent and summed in bfloat16 or wider, within the bound.
A program may use at most 64 MiB of HBM per device.

v0:
```python
import math
import jax
import jax.numpy as jnp
from jax import lax
from jax.sharding import PartitionSpec as P

FOCUS_NUMBER = 8
FOCUS_BREADTH = 32
COUPLING_DIM = 32
epsilon = 1e-05
mask_fill = 1000000000.0


def layer_norm(values):
    centre = values - jnp.mean(values, axis=-1, keepdims=True)
    spread = jnp.mean(centre * centre, axis=-1, keepdims=True)
    return centre * lax.rsqrt(spread + epsilon)


def column_delta(block, row_present_flags, attention_weights):
    (
        query_weight,
        key_weight,
        content_matrix,
        sigmoid_switch_matrix,
        focus_merge_matrix,
        widening_matrix,
        narrowing_matrix,
        first_factor_matrix,
        second_factor_matrix,
    ) = attention_weights
    row_count, item_count, channel_width = block.shape
    inputs = block.astype(jnp.float32)
    normed = layer_norm(inputs).astype(jnp.bfloat16)
    scaling = 1.0 / math.sqrt(FOCUS_BREADTH)
    queries = (jnp.dot(normed, query_weight, preferred_element_type=jnp.float32) * scaling).astype(
        jnp.bfloat16
    )
    queries = queries.reshape(row_count, item_count, FOCUS_NUMBER, FOCUS_BREADTH)
    keys_all = jnp.dot(normed, key_weight, preferred_element_type=jnp.float32).astype(jnp.bfloat16)
    keys_all = keys_all.reshape(row_count, item_count, FOCUS_NUMBER, FOCUS_BREADTH)
    values_all = jnp.dot(normed, content_matrix, preferred_element_type=jnp.float32).astype(
        jnp.bfloat16
    )
    values_all = values_all.reshape(row_count, item_count, FOCUS_NUMBER, FOCUS_BREADTH)
    gate_values = jax.nn.sigmoid(
        jnp.dot(normed, sigmoid_switch_matrix, preferred_element_type=jnp.float32)
    )
    scores = jnp.einsum("skhd,tkhd->khst", queries, keys_all, preferred_element_type=jnp.float32)
    scores = scores + ((row_present_flags - 1.0) * mask_fill)[None, None, None, :]
    peak_score = jnp.max(scores, axis=-1, keepdims=True)
    exponent = jnp.exp(scores - peak_score)
    probs = (exponent / jnp.sum(exponent, axis=-1, keepdims=True)).astype(jnp.bfloat16)
    attended = jnp.einsum("khst,tkhd->skhd", probs, values_all, preferred_element_type=jnp.float32)
    attended = attended.reshape(row_count, item_count, FOCUS_NUMBER * FOCUS_BREADTH)
    gated = (gate_values * attended).astype(jnp.bfloat16)
    after_attn = (
        inputs + jnp.dot(gated, focus_merge_matrix, preferred_element_type=jnp.float32)
    ).astype(jnp.bfloat16)
    normed_two = layer_norm(after_attn.astype(jnp.float32)).astype(jnp.bfloat16)
    hidden = jax.nn.relu(
        jnp.dot(normed_two, widening_matrix, preferred_element_type=jnp.float32)
    ).astype(jnp.bfloat16)
    after_trans = (
        after_attn.astype(jnp.float32)
        + jnp.dot(hidden, narrowing_matrix, preferred_element_type=jnp.float32)
    ).astype(jnp.bfloat16)
    normed_three = layer_norm(after_trans.astype(jnp.float32)).astype(jnp.bfloat16)
    row_scale = row_present_flags[:, None, None]
    left_proj = (
        jnp.dot(normed_three, first_factor_matrix, preferred_element_type=jnp.float32) * row_scale
    ).astype(jnp.bfloat16)
    right_proj = (
        jnp.dot(normed_three, second_factor_matrix, preferred_element_type=jnp.float32) * row_scale
    ).astype(jnp.bfloat16)
    return (after_trans, left_proj, right_proj)


def pair_block_update(
    left_rows,
    right_full,
    pair_block,
    norm_block,
    outer_product_weight,
    outer_product_bias,
    pair_up_weight,
    pair_down_weight,
):
    outer = jnp.einsum(
        "sic,sje->ijce", left_rows, right_full, preferred_element_type=jnp.float32
    ).astype(jnp.bfloat16)
    row_span, column_extent = norm_block.shape
    flat = outer.reshape(row_span, column_extent, COUPLING_DIM * COUPLING_DIM)
    projected = (
        jnp.dot(flat, outer_product_weight, preferred_element_type=jnp.float32) + outer_product_bias
    )
    outer_mean = projected / jnp.maximum(norm_block, 1.0)[:, :, None]
    pair_mid = (pair_block.astype(jnp.float32) + outer_mean).astype(jnp.bfloat16)
    normed = layer_norm(pair_mid.astype(jnp.float32)).astype(jnp.bfloat16)
    hidden = jax.nn.relu(
        jnp.dot(normed, pair_up_weight, preferred_element_type=jnp.float32)
    ).astype(jnp.bfloat16)
    return (
        pair_mid.astype(jnp.float32)
        + jnp.dot(hidden, pair_down_weight, preferred_element_type=jnp.float32)
    ).astype(jnp.bfloat16)


def per_device(
    homolog_embedding,
    pair_features,
    row_present_mask,
    residue_keep_mask,
    query_weight,
    key_weight,
    content_matrix,
    sigmoid_switch_matrix,
    focus_merge_matrix,
    widening_matrix,
    narrowing_matrix,
    first_factor_matrix,
    second_factor_matrix,
    outer_product_weight,
    outer_product_bias,
    pair_up_weight,
    pair_down_weight,
):
    seq_count = lax.axis_size("seq")
    res_count = lax.axis_size("res")
    seq_index = lax.axis_index("seq")
    res_index = lax.axis_index("res")
    shard_rows, column_extent, channel_width = homolog_embedding.shape
    residue_total = column_extent * res_count
    row_span = residue_total // seq_count
    owned_columns = column_extent // seq_count
    row_present_flags = row_present_mask.astype(jnp.float32)
    attention_weights = (
        query_weight,
        key_weight,
        content_matrix,
        sigmoid_switch_matrix,
        focus_merge_matrix,
        widening_matrix,
        narrowing_matrix,
        first_factor_matrix,
        second_factor_matrix,
    )
    grouped = homolog_embedding.reshape(shard_rows, seq_count, owned_columns, channel_width)
    flat_block = lax.all_to_all(grouped, "seq", split_axis=1, concat_axis=0, tiled=True)[:, 0]
    after_trans, left_proj, right_proj = column_delta(
        flat_block, row_present_flags, attention_weights
    )
    alignment_columns = after_trans[:, None]
    left_column_set = left_proj[:, None]
    right_column_set = right_proj[:, None]
    alignment_columns = alignment_columns[:, 0]
    left_column_set = left_column_set[:, 0]
    right_column_set = right_column_set[:, 0]
    alignment_output, left_home = (
        lax.all_to_all(alignment_columns, "seq", split_axis=0, concat_axis=1, tiled=True),
        lax.all_to_all(left_column_set, "seq", split_axis=0, concat_axis=1, tiled=True),
    )
    right_full = lax.all_gather(right_column_set, "seq", axis=1, tiled=True)
    left_wide = lax.all_gather(left_home, "res", axis=1, tiled=True)
    left_rows = lax.all_to_all(left_wide, "seq", split_axis=1, concat_axis=0, tiled=True)
    row_res = lax.dynamic_slice_in_dim(residue_keep_mask, seq_index * row_span, row_span, 0)
    col_res = lax.dynamic_slice_in_dim(
        residue_keep_mask, res_index * column_extent, column_extent, 0
    )
    left_rows = left_rows * row_res.astype(jnp.bfloat16)[None, :, None]
    right_full = right_full * col_res.astype(jnp.bfloat16)[None, :, None]
    live_rows = jnp.sum(row_present_flags)
    norm_tile = (
        live_rows * row_res.astype(jnp.float32)[:, None] * col_res.astype(jnp.float32)[None, :]
    )
    overall_rows = left_rows.shape[0]
    block_rows = math.gcd(row_span, 8)
    block_count = row_span // block_rows
    left_groups = left_rows.reshape(overall_rows, block_count, block_rows, COUPLING_DIM).transpose(
        1, 0, 2, 3
    )
    pair_groups = pair_features.reshape(
        block_count, block_rows, column_extent, pair_features.shape[2]
    )
    norm_groups = norm_tile.reshape(block_count, block_rows, column_extent)

    def per_rows(pieces):
        left_block, pair_block, norm_block = pieces
        return pair_block_update(
            left_block,
            right_full,
            pair_block,
            norm_block,
            outer_product_weight,
            outer_product_bias,
            pair_up_weight,
            pair_down_weight,
        )

    pair_output = lax.map(per_rows, (left_groups, pair_groups, norm_groups))
    pair_output = pair_output.reshape(row_span, column_extent, pair_features.shape[2])
    return (alignment_output, pair_output)


def solution(mesh):
    placed = (
        P("seq", "res", None),
        P("seq", "res", None),
        P(),
        P(),
        P(),
        P(),
        P(),
        P(),
        P(),
        P(),
        P(),
        P(),
        P(),
        P(),
        P(),
        P(),
        P(),
    )
    return jax.shard_map(
        per_device,
        mesh=mesh,
        in_specs=placed,
        out_specs=(P("seq", "res", None), P("seq", "res", None)),
        check_vma=False,
    )
```

profile of v0, /device:TPU:0, one launch (start us, length us, event | category | flops | bytes accessed | tf_op | source)
XLA Modules:
  0.0 129.4 jit_solution(13391735593208518622)
XLA Ops:
  7.2 2.2 %copy.150 = bf16[16,64,256]{2,0,1:T(8,128)(2,1)} copy(bf16[16,64,256]{2,1,0:T(8,128)(2,1)} %param.17) | data formatting | bytes 1048576 | tf_op args[0]
  9.4 7.4 %all-to-all-start = ((bf16[16,16,4,256]{3,0,2,1:T(8,128)(2,1)}), bf16[16,16,4,256]{3,0,2,1:T(8,128)(2,1)S(1)}, u32[]{:S(2)}, u32[]{:S(2)}) async-start(bf16[16,16,4,256]{3,0,2,1:T(8,128)(2,1)} %bitcast), calls=%async_computation | async-start | bytes 1048576 | tf_op jit(solution)/shard_map/all_to_all | solution.py:149
  16.8 0.7 convert_element_type.120
  17.5 1.3 %convert_reduce_fusion.2 = (f32[]{:T(128)}, f32[256]{0:T(256)S(1)}) fusion(s32[256]{0:T(256)} %param.19), kind=kLoop, calls=%fused_computation.96 | loop fusion | flops 1023 | bytes 2052 | tf_op jit(solution)/shard_map/reduce_sum | solution.py:172
  18.9 12.2 %all-to-all-done = bf16[16,16,4,256]{3,0,2,1:T(8,128)(2,1)S(1)} async-done(((bf16[16,16,4,256]{3,0,2,1:T(8,128)(2,1)}), bf16[16,16,4,256]{3,0,2,1:T(8,128)(2,1)S(1)}, u32[]{:S(2)}, u32[]{:S(2)}) %all-to-all-start) | async-done | bytes 524320 | tf_op jit(solution)/shard_map/all_to_all | solution.py:149
  31.1 0.2 fusion.39
  31.3 0.1 div.52
  31.4 0.4 multiply_reduce_fusion
  31.9 0.1 rsqrt.37
  32.0 0.1 convert_bitcast_fusion.1
  32.1 0.1 copy.151
  32.2 0.3 copy.161
  32.5 0.3 multiply_convert_fusion
  32.9 0.3 convolution_convert_fusion
  33.3 1.1 fusion.14
  34.4 0.3 convolution_convert_fusion.1
  34.8 7.0 %fusion.74 = (f32[4,8,256]{2,1,0:T(8,128)S(1)}, f32[4,8,256,256]{2,3,1,0:T(8,128)}) fusion(f32[256]{0:T(256)S(1)} %get-tuple-element.43, bf16[256,4,8,32]{0,3,2,1:T(8,128)(2,1)} %bitcast.120, bf16[256,4,8,32]{0,3,2,1:T(8,128)(2,1)S(1)} %bitcast.119), kind=kOutput, calls=%fused_computation.100 | convolution fusion | flops 140509440 | bytes 9470976 | tf_op jit(solution)/shard_map/sub | solution.py:52
  41.8 5.3 %fusion.5 = f32[4,8,32,256]{3,2,1,0:T(8,128)} fusion(bf16[256,4,8,32]{0,3,2,1:T(8,128)(2,1)S(1)} %bitcast.118, f32[4,8,256,256]{2,3,1,0:T(8,128)} %get-tuple-element.47, f32[4,8,256]{2,1,0:T(8,128)S(1)} %get-tuple-element.46), kind=kOutput, calls=%fused_computation.8 | convolution fusion | flops 138412032 | bytes 9994240 | tf_op jit(solution)/shard_map/khst,tkhd->skhd/dot_general | solution.py:54
  47.1 1.6 %copy.159 = f32[256,4,256]{2,0,1:T(8,128)S(1)} copy(f32[256,4,256]{0,2,1:T(8,128)} %bitcast.116) | data formatting | bytes 2097152 | tf_op jit(solution)/shard_map/reshape | solution.py:55
  48.7 1.4 %convert_reduce_fusion = (f32[256,4]{0,1:T(4,128)S(1)}, bf16[256,4,256]{0,2,1:T(8,128)(2,1)}) fusion(f32[256,4,256]{0,2,1:T(8,128)S(1)} %copy.161, bf16[256,256]{1,0:T(8,128)(2,1)S(1)} %copy-done.6, f32[256,4,256]{2,0,1:T(8,128)S(1)} %copy.159, bf16[256,4,256]{2,0,1:T(8,128)(2,1)S(1)} %multiply_convert_fusion, bf16[256,256]{1,0:T(8,128)(2,1)S(1)} %copy-done.7), kind=kOutput, calls=%fused_computation.12 | convolution fusion | flops 270793728 | bytes 3411968 | tf_op jit(solution)/shard_map/dot_general | solution.py:58
  50.1 1.2 fusion.29
  51.4 2.7 %convert_reduce_fusion.1 = (f32[256,4]{0,1:T(4,128)S(1)}, bf16[256,4,256]{0,2,1:T(8,128)(2,1)S(1)}) fusion(bf16[1024,256]{1,0:T(8,128)(2,1)S(1)} %copy-done, bf16[256,4,256]{0,2,1:T(8,128)(2,1)} %get-tuple-element.49, bf16[256,1024]{1,0:T(8,128)(2,1)} %param.26, f32[256,4]{0,1:T(4,128)S(1)} %add_rsqrt_fusion.2, f32[256,4]{0,1:T(4,128)S(1)} %broadcast_multiply_fusion.2), kind=kOutput, calls=%fused_computation.22 | convolution fusion | flops 1078197248 | bytes 2109440 | tf_op jit(solution)/shard_map/dot_general | solution.py:66
  54.1 0.2 fusion.31
  54.2 0.9 fusion.27
  55.1 0.3 fusion.28
  55.4 0.2 copy.169
  55.6 0.3 reshape.153
  55.9 10.9 %all_to_all.63 = bf16[16,2,1024]{2,1,0:T(2,128)(2,1)S(1)} all-to-all(bf16[16,2,1024]{2,1,0:T(2,128)(2,1)S(1)} %reshape.153), channel_id=1, replica_groups=mesh['seq'=16,'res'=2] {'seq'}, dimensions={0} | all-to-all | bytes 131072 | tf_op jit(solution)/shard_map/all_to_all | solution.py:161
  66.7 0.2 reshape.154
  67.0 8.4 %all_gather.7 = bf16[16,128,32]{2,0,1:T(8,128)(2,1)S(1)} all-gather(bf16[16,64,32]{2,0,1:T(8,128)(2,1)S(1)} %bitcast.115), channel_id=1, replica_groups=mesh['seq'=16,'res'=2] {'res'}, dimensions={1}, use_global_device_ids=true | all-gather | bytes 196608 | tf_op jit(solution)/shard_map/all_gather | solution.py:164
  75.4 1.2 reshape.155
  76.6 3.5 %all-to-all-start.3 = ((bf16[16,2,2048]{2,1,0:T(2,128)(2,1)}), bf16[16,2,2048]{2,1,0:T(2,128)(2,1)S(1)}, u32[]{:S(2)}, u32[]{:S(2)}) async-start(bf16[16,2,2048]{2,1,0:T(2,128)(2,1)} %reshape.155), calls=%async_computation.3 | async-start | bytes 262144 | tf_op jit(solution)/shard_map/all_to_all | solution.py:165
  80.1 1.1 copy.164
  81.2 8.0 %all-to-all-done.3 = bf16[16,2,2048]{2,1,0:T(2,128)(2,1)S(1)} async-done(((bf16[16,2,2048]{2,1,0:T(2,128)(2,1)}), bf16[16,2,2048]{2,1,0:T(2,128)(2,1)S(1)}, u32[]{:S(2)}, u32[]{:S(2)}) %all-to-all-start.3) | async-done | bytes 131104 | tf_op jit(solution)/shard_map/all_to_all | solution.py:165
  89.1 3.8 %all-to-all-start.1 = ((bf16[256,4,256]{2,1,0:T(4,128)(2,1)}), bf16[256,4,256]{2,1,0:T(4,128)(2,1)S(1)}, u32[]{:S(2)}, u32[]{:S(2)}) async-start(bf16[256,4,256]{2,1,0:T(4,128)(2,1)} %copy.164), calls=%async_computation.1 | async-start | bytes 1048576 | tf_op jit(solution)/shard_map/all_to_all | solution.py:160
  92.9 0.1 dynamic-slice_convert_fusion
  93.0 0.7 convert_multiply_fusion
  93.9 0.3 reshape.156
  94.1 0.1 copy.173
  94.3 0.1 bitcast_multiply_fusion
  94.4 0.3 copy.174
  94.7 12.2 %all-to-all-done.1 = bf16[256,4,256]{2,1,0:T(4,128)(2,1)S(1)} async-done(((bf16[256,4,256]{2,1,0:T(4,128)(2,1)}), bf16[256,4,256]{2,1,0:T(4,128)(2,1)S(1)}, u32[]{:S(2)}, u32[]{:S(2)}) %all-to-all-start.1) | async-done | bytes 524320 | tf_op jit(solution)/shard_map/all_to_all | solution.py:160
  107.1 1.0 copy.177
  108.1 4.4 %convert_bitcast_fusion = bf16[8,64,32,32]{2,3,0,1:T(8,128)(2,1)} fusion(bf16[256,64,32]{0,2,1:T(8,128)(2,1)} %all-gather.2.cloned.1.call-done, bf16[64]{0:T(256)(128)(2,1)S(1)} %get-tuple-element.45, bf16[256,8,32]{0,2,1:T(8,128)(2,1)S(1)} %copy.174), kind=kOutput, calls=%fused_computation.5 | convolution fusion | flops 271056896 | bytes 2228352 | tf_op jit(solution)/shard_map/while/body/eval_jaxpr/sic,sje->ijce/dot_general | solution.py:89
  112.5 7.7 %copy.175 = bf16[8,64,32,32]{1,3,2,0:T(8,128)(2,1)S(1)} copy(bf16[8,64,32,32]{2,3,0,1:T(8,128)(2,1)} %convert_bitcast_fusion) | data formatting | bytes 2097152 | tf_op jit(solution)/shard_map/while/body/eval_jaxpr/convert_element_type | solution.py:91
  120.3 0.8 fusion.81
  121.1 0.3 multiply_reduce_fusion.1
  121.4 1.2 fusion.26
  (46 shorter events, 0.5 us)
Async XLA Ops:
  7.2 44.2 %copy-start = (bf16[1024,256]{1,0:T(8,128)(2,1)S(1)}, bf16[1024,256]{1,0:T(8,128)(2,1)}, u32[]{:S(2)}) copy-start(bf16[1024,256]{1,0:T(8,128)(2,1)} %param.27) | copy-start | bytes 1572868
  9.4 21.7 %all-to-all-start = ((bf16[16,16,4,256]{3,0,2,1:T(8,128)(2,1)}), bf16[16,16,4,256]{3,0,2,1:T(8,128)(2,1)S(1)}, u32[]{:S(2)}, u32[]{:S(2)}) async-start(bf16[16,16,4,256]{3,0,2,1:T(8,128)(2,1)} %bitcast), calls=%async_computation | async-start | bytes 1048576 | tf_op jit(solution)/shard_map/all_to_all | solution.py:149
  16.8 91.3 %all-gather.2.cloned.1.call-start = ((), (), s32[]{:S(2)}) async-start(), calls=%async_computation.4 | async-start | bytes 1114112 | tf_op jit(solution)/shard_map/all_gather | solution.py:163
  31.3 1.6 %copy-start.1 = (bf16[256,256]{1,0:T(8,128)(2,1)S(1)}, bf16[256,256]{1,0:T(8,128)(2,1)}, u32[]{:S(2)}) copy-start(bf16[256,256]{1,0:T(8,128)(2,1)} %param.22) | copy-start | bytes 393220
  32.0 1.3 copy-start.2
  32.1 2.3 %copy-start.3 = (bf16[256,256]{1,0:T(8,128)(2,1)S(1)}, bf16[256,256]{1,0:T(8,128)(2,1)}, u32[]{:S(2)}) copy-start(bf16[256,256]{1,0:T(8,128)(2,1)} %param.23) | copy-start | bytes 393220
  41.8 6.9 %copy-start.6 = (bf16[256,256]{1,0:T(8,128)(2,1)S(1)}, bf16[256,256]{1,0:T(8,128)(2,1)}, u32[]{:S(2)}) copy-start(bf16[256,256]{1,0:T(8,128)(2,1)} %param.25) | copy-start | bytes 393220
  41.8 6.9 %copy-start.7 = (bf16[256,256]{1,0:T(8,128)(2,1)S(1)}, bf16[256,256]{1,0:T(8,128)(2,1)}, u32[]{:S(2)}) copy-start(bf16[256,256]{1,0:T(8,128)(2,1)} %param.24) | copy-start | bytes 393220
  50.1 4.1 %copy-start.11 = (bf16[256,32]{0,1:T(8,128)(2,1)S(1)}, bf16[256,32]{0,1:T(8,128)(2,1)}, u32[]{:S(2)}) copy-start(bf16[256,32]{0,1:T(8,128)(2,1)} %param.29) | copy-start | bytes 49156
  50.1 5.0 %copy-start.12 = (bf16[256,32]{0,1:T(8,128)(2,1)S(1)}, bf16[256,32]{0,1:T(8,128)(2,1)}, u32[]{:S(2)}) copy-start(bf16[256,32]{0,1:T(8,128)(2,1)} %param.28) | copy-start | bytes 49156
  54.0 38.9 %copy-start.4 = (s32[128]{0:T(128)S(1)}, s32[128]{0:T(128)}, u32[]{:S(2)}) copy-start(s32[128]{0:T(128)} %param.20) | copy-start | bytes 1540
  76.6 12.5 %all-to-all-start.3 = ((bf16[16,2,2048]{2,1,0:T(2,128)(2,1)}), bf16[16,2,2048]{2,1,0:T(2,128)(2,1)S(1)}, u32[]{:S(2)}, u32[]{:S(2)}) async-start(bf16[16,2,2048]{2,1,0:T(2,128)(2,1)} %reshape.155), calls=%async_computation.3 | async-start | bytes 262144 | tf_op jit(solution)/shard_map/all_to_all | solution.py:165
  89.1 17.8 %all-to-all-start.1 = ((bf16[256,4,256]{2,1,0:T(4,128)(2,1)}), bf16[256,4,256]{2,1,0:T(4,128)(2,1)S(1)}, u32[]{:S(2)}, u32[]{:S(2)}) async-start(bf16[256,4,256]{2,1,0:T(4,128)(2,1)} %copy.164), calls=%async_computation.1 | async-start | bytes 1048576 | tf_op jit(solution)/shard_map/all_to_all | solution.py:160
  112.5 7.7 %copy-start.5 = (bf16[1024,128]{1,0:T(8,128)(2,1)S(1)}, bf16[1024,128]{1,0:T(8,128)(2,1)}, u32[]{:S(2)}) copy-start(bf16[1024,128]{1,0:T(8,128)(2,1)} %param.30) | copy-start | bytes 786436
  112.5 7.7 %copy-start.8 = (bf16[8,64,128]{2,1,0:T(8,128)(2,1)S(1)}, bf16[8,64,128]{2,1,0:T(8,128)(2,1)}, u32[]{:S(2)}) copy-start(bf16[8,64,128]{2,1,0:T(8,128)(2,1)} %param.18) | copy-start | bytes 393220
  112.5 7.7 %copy-start.13 = (f32[128]{0:T(128)S(1)}, f32[128]{0:T(128)}, u32[]{:S(2)}) copy-start(f32[128]{0:T(128)} %param.31) | copy-start | bytes 1540
  112.5 8.9 %copy-start.9 = (bf16[512,128]{1,0:T(8,128)(2,1)S(1)}, bf16[512,128]{1,0:T(8,128)(2,1)}, u32[]{:S(2)}) copy-start(bf16[512,128]{1,0:T(8,128)(2,1)} %param.33) | copy-start | bytes 393220
  112.5 8.9 %copy-start.10 = (bf16[128,512]{1,0:T(8,128)(2,1)S(1)}, bf16[128,512]{1,0:T(8,128)(2,1)}, u32[]{:S(2)}) copy-start(bf16[128,512]{1,0:T(8,128)(2,1)} %param.32) | copy-start | bytes 393220
Sparse Core Ops, SparseCore 0:
  55.3 37.4 all-gather.1
where the time goes:
time: 130 us; the launch traced here: 129 us
  waiting for transfers between devices  32.4 us (25%)
  matrix products  25.8 us (20%)
  blocking collectives  19.3 us (15%)
  local copies, waits for them, and re-layouts  16.8 us (13%)
  starting transfers between devices  14.7 us (11%)
  between operations  14.4 us (11%)
  other arithmetic  5.9 us (5%)
    all_to_all x1, waiting for transfers between devices, per_device(): lax.all_to_all(alignment_columns, 'seq', split_axis=0, concat_axis=1, til...  12.2 us
    all_to_all x1, waiting for transfers between devices, per_device(): lax.all_to_all(grouped, 'seq', split_axis=1, concat_axis=0, tiled=True)  12.2 us
    all_to_all x1, blocking collectives, per_device(): lax.all_to_all(left_column_set, 'seq', split_axis=0, concat_axis=1, tiled...  10.9 us
    all_gather x1, blocking collectives, per_device(): left_wide = lax.all_gather(left_home, 'res', axis=1, tiled=True)  8.43 us
    all_to_all x1, waiting for transfers between devices, per_device(): lax.all_to_all(left_wide, 'seq', split_axis=1, concat_axis=0, tiled=True)  7.96 us
    convert_element_type x1, local copies, waits for them, and re-layouts, pair_block_update(): outer = jnp.einsum('sic,sje->ijce', left_rows, right_full, preferred_elem...  7.69 us
    all_to_all x1, starting transfers between devices, per_device(): lax.all_to_all(grouped, 'seq', split_axis=1, concat_axis=0, tiled=True)  7.41 us
    sub x1, matrix products, column_delta(): exponent = jnp.exp(scores - peak_score)  7.03 us
  transfers between devices with their start and end apart: 4, of which 3 were waited for; matrix products, arithmetic and copies ran while one was open for 6% of the time, Pallas kernels for 0%

commit v1 on v0

--- a/solution.py
+++ b/solution.py
@@ -146,7 +146,10 @@
         second_factor_matrix,
     )
     grouped = homolog_embedding.reshape(shard_rows, seq_count, owned_columns, channel_width)
-    flat_block = lax.all_to_all(grouped, "seq", split_axis=1, concat_axis=0, tiled=True)[:, 0]
+    flat_block = jnp.concatenate(
+        lax.all_to_all(jnp.stack(jnp.split(grouped, lax.axis_size("seq"), axis=1)), "seq", 0, 0),
+        axis=0,
+    )[:, 0]
     after_trans, left_proj, right_proj = column_delta(
         flat_block, row_present_flags, attention_weights
     )

time: 130 us -> 139 us (1.069)
  local copies, waits for them, and re-layouts: 16.8 us -> 26 us
    unnamed x34 -> x49, local copies, waits for them, and re-layouts: 5.11 us -> 13.6 us
where the time goes in v1:
time: 139 us
  waiting for transfers between devices  32.4 us (23%)
  local copies, waits for them, and re-layouts  26 us (19%)
  matrix products  25.8 us (19%)
  blocking collectives  19.3 us (14%)
  starting transfers between devices  14.9 us (11%)
  between operations  14.4 us (10%)
  other arithmetic  5.77 us (4%)
    unnamed x49, local copies, waits for them, and re-layouts  13.6 us
    all_to_all x1, waiting for transfers between devices, per_device(): lax.all_to_all(alignment_columns, 'seq', split_axis=0, concat_axis=1, til...  12.2 us
    all_to_all x1, waiting for transfers between devices, per_device(): lax.all_to_all(jnp.stack(jnp.split(grouped, lax.axis_size('seq'), axis=1)...  12.2 us
    all_to_all x1, blocking collectives, per_device(): lax.all_to_all(left_column_set, 'seq', split_axis=0, concat_axis=1, tiled...  10.9 us
    all_gather x1, blocking collectives, per_device(): left_wide = lax.all_gather(left_home, 'res', axis=1, tiled=True)  8.43 us
    all_to_all x1, waiting for transfers between devices, per_device(): lax.all_to_all(left_wide, 'seq', split_axis=1, concat_axis=0, tiled=True)  7.96 us
    convert_element_type x1, local copies, waits for them, and re-layouts, pair_block_update(): outer = jnp.einsum('sic,sje->ijce', left_rows, right_full, preferred_elem...  7.69 us
    all_to_all x1, starting transfers between devices, per_device(): lax.all_to_all(jnp.stack(jnp.split(grouped, lax.axis_size('seq'), axis=1)...  7.55 us
  transfers between devices with their start and end apart: 4, of which 3 were waited for; matrix products, arithmetic and copies ran while one was open for 6% of the time, Pallas kernels for 0%

profile of v1, /device:TPU:0, one launch (start us, length us, event | category | flops | bytes accessed | tf_op | source)
XLA Modules:
  0.0 138.5 jit_solution(10299040306327371390)
XLA Ops:
  7.2 1.4 %copy.168 = bf16[16,64,256]{2,0,1:T(8,128)(2,1)S(1)} copy(bf16[16,64,256]{2,1,0:T(8,128)(2,1)} %param.17) | data formatting | bytes 1048576 | tf_op args[0]
  8.6 0.6 constant_dynamic-update-slice_fusion.15
  9.2 0.6 constant_dynamic-update-slice_fusion.14
  9.8 0.6 constant_dynamic-update-slice_fusion.13
  10.4 0.6 constant_dynamic-update-slice_fusion.12
  11.0 0.6 constant_dynamic-update-slice_fusion.11
  11.7 0.6 constant_dynamic-update-slice_fusion.10
  12.3 0.6 constant_dynamic-update-slice_fusion.9
  12.9 0.6 constant_dynamic-update-slice_fusion.8
  13.5 0.6 constant_dynamic-update-slice_fusion.7
  14.1 0.6 constant_dynamic-update-slice_fusion.6
  14.7 0.6 constant_dynamic-update-slice_fusion.5
  15.4 0.6 constant_dynamic-update-slice_fusion.4
  16.0 0.6 constant_dynamic-update-slice_fusion.3
  16.6 0.6 constant_dynamic-update-slice_fusion.2
  17.2 0.6 constant_dynamic-update-slice_fusion.1
  17.8 0.6 constant_dynamic-update-slice_fusion
  18.5 7.5 %all-to-all-start = ((bf16[16,16,1,4,256]{4,1,3,2,0:T(8,128)(2,1)}), bf16[16,16,1,4,256]{4,1,3,2,0:T(8,128)(2,1)S(1)}, u32[]{:S(2)}, u32[]{:S(2)}) async-start(bf16[16,16,1,4,256]{4,1,3,2,0:T(8,128)(2,1)} %constant_dynamic-update-slice_fusion), calls=%async_computation | async-start | bytes 1048576 | tf_op jit(solution)/shard_map/all_to_all | solution.py:150
  26.1 0.7 convert_element_type.110
  26.7 1.3 convert_reduce_fusion.3
  28.1 12.2 %all-to-all-done = bf16[16,16,1,4,256]{4,1,3,2,0:T(8,128)(2,1)S(1)} async-done(((bf16[16,16,1,4,256]{4,1,3,2,0:T(8,128)(2,1)}), bf16[16,16,1,4,256]{4,1,3,2,0:T(8,128)(2,1)S(1)}, u32[]{:S(2)}, u32[]{:S(2)}) %all-to-all-start) | async-done | bytes 524320 | tf_op jit(solution)/shard_map/all_to_all | solution.py:150
  40.7 0.4 multiply_reduce_fusion
  41.3 0.3 copy.179
  41.7 0.3 multiply_convert_fusion
  42.0 0.3 fusion.14
  42.4 1.1 convolution_convert_fusion
  43.5 0.3 convolution_convert_fusion.1
  43.9 7.0 %fusion.73 = (f32[4,8,256]{2,1,0:T(8,128)S(1)}, f32[4,8,256,256]{2,3,1,0:T(8,128)}) fusion(f32[256]{0:T(256)S(1)} %get-tuple-element.43, bf16[256,4,8,32]{0,3,2,1:T(8,128)(2,1)S(1)} %bitcast.188, bf16[256,4,8,32]{0,3,2,1:T(8,128)(2,1)} %bitcast.189), kind=kOutput, calls=%fused_computation.131 | convolution fusion | flops 140509440 | bytes 9470976 | tf_op jit(solution)/shard_map/sub | solution.py:52
  50.9 5.3 %fusion.5 = f32[4,8,32,256]{3,2,1,0:T(8,128)} fusion(bf16[256,4,8,32]{0,3,2,1:T(8,128)(2,1)S(1)} %bitcast.187, f32[4,8,256,256]{2,3,1,0:T(8,128)} %get-tuple-element.47, f32[4,8,256]{2,1,0:T(8,128)S(1)} %get-tuple-element.46), kind=kOutput, calls=%fused_computation.8 | convolution fusion | flops 138412032 | bytes 9994240 | tf_op jit(solution)/shard_map/khst,tkhd->skhd/dot_general | solution.py:54
  56.2 1.6 %copy.177 = f32[256,4,256]{2,0,1:T(8,128)S(1)} copy(f32[256,4,256]{0,2,1:T(8,128)} %bitcast.185) | data formatting | bytes 2097152 | tf_op jit(solution)/shard_map/reshape | solution.py:55
  57.8 1.4 %convert_reduce_fusion = (f32[256,4]{0,1:T(4,128)S(1)}, bf16[256,4,256]{0,2,1:T(8,128)(2,1)}) fusion(f32[256,4,256]{0,2,1:T(8,128)S(1)} %copy.179, bf16[256,256]{1,0:T(8,128)(2,1)S(1)} %copy-done.6, f32[256,4,256]{2,0,1:T(8,128)S(1)} %copy.177, bf16[256,4,256]{2,0,1:T(8,128)(2,1)S(1)} %multiply_convert_fusion, bf16[256,256]{1,0:T(8,128)(2,1)S(1)} %copy-done.7), kind=kOutput, calls=%fused_computation.12 | convolution fusion | flops 270793728 | bytes 3411968 | tf_op jit(solution)/shard_map/dot_general | solution.py:58
  59.2 1.2 fusion.29
  60.5 2.7 %convert_reduce_fusion.1 = (f32[256,4]{0,1:T(4,128)S(1)}, bf16[256,4,256]{0,2,1:T(8,128)(2,1)S(1)}) fusion(bf16[1024,256]{1,0:T(8,128)(2,1)S(1)} %copy-done, bf16[256,4,256]{0,2,1:T(8,128)(2,1)} %get-tuple-element.49, bf16[256,1024]{1,0:T(8,128)(2,1)} %param.26, f32[256,4]{0,1:T(4,128)S(1)} %add_rsqrt_fusion.2, f32[256,4]{0,1:T(4,128)S(1)} %broadcast_multiply_fusion.2), kind=kOutput, calls=%fused_computation.22 | convolution fusion | flops 1078197248 | bytes 2109440 | tf_op jit(solution)/shard_map/dot_general | solution.py:66
  63.4 0.9 fusion.27
  65.0 10.9 %all_to_all.59 = bf16[16,2,1024]{2,1,0:T(2,128)(2,1)S(1)} all-to-all(bf16[16,2,1024]{2,1,0:T(2,128)(2,1)S(1)} %reshape.146), channel_id=1, replica_groups=mesh['seq'=16,'res'=2] {'seq'}, dimensions={0} | all-to-all | bytes 131072 | tf_op jit(solution)/shard_map/all_to_all | solution.py:164
  76.1 8.4 %all_gather.7 = bf16[16,128,32]{2,0,1:T(8,128)(2,1)S(1)} all-gather(bf16[16,64,32]{2,0,1:T(8,128)(2,1)S(1)} %bitcast.184), channel_id=1, replica_groups=mesh['seq'=16,'res'=2] {'res'}, dimensions={1}, use_global_device_ids=true | all-gather | bytes 196608 | tf_op jit(solution)/shard_map/all_gather | solution.py:167
  84.6 1.2 reshape.148
  85.7 3.5 %all-to-all-start.3 = ((bf16[16,2,2048]{2,1,0:T(2,128)(2,1)}), bf16[16,2,2048]{2,1,0:T(2,128)(2,1)S(1)}, u32[]{:S(2)}, u32[]{:S(2)}) async-start(bf16[16,2,2048]{2,1,0:T(2,128)(2,1)} %reshape.148), calls=%async_computation.3 | async-start | bytes 262144 | tf_op jit(solution)/shard_map/all_to_all | solution.py:168
  89.3 1.1 copy.182
  90.3 8.0 %all-to-all-done.3 = bf16[16,2,2048]{2,1,0:T(2,128)(2,1)S(1)} async-done(((bf16[16,2,2048]{2,1,0:T(2,128)(2,1)}), bf16[16,2,2048]{2,1,0:T(2,128)(2,1)S(1)}, u32[]{:S(2)}, u32[]{:S(2)}) %all-to-all-start.3) | async-done | bytes 131104 | tf_op jit(solution)/shard_map/all_to_all | solution.py:168
  98.3 3.8 %all-to-all-start.1 = ((bf16[256,4,256]{2,1,0:T(4,128)(2,1)}), bf16[256,4,256]{2,1,0:T(4,128)(2,1)S(1)}, u32[]{:S(2)}, u32[]{:S(2)}) async-start(bf16[256,4,256]{2,1,0:T(4,128)(2,1)} %copy.182), calls=%async_computation.1 | async-start | bytes 1048576 | tf_op jit(solution)/shard_map/all_to_all | solution.py:163
  102.1 0.7 convert_multiply_fusion
  103.9 12.2 %all-to-all-done.1 = bf16[256,4,256]{2,1,0:T(4,128)(2,1)S(1)} async-done(((bf16[256,4,256]{2,1,0:T(4,128)(2,1)}), bf16[256,4,256]{2,1,0:T(4,128)(2,1)S(1)}, u32[]{:S(2)}, u32[]{:S(2)}) %all-to-all-start.1) | async-done | bytes 524320 | tf_op jit(solution)/shard_map/all_to_all | solution.py:163
  116.2 1.0 copy.195
  117.2 4.4 %convert_bitcast_fusion = bf16[8,64,32,32]{2,3,0,1:T(8,128)(2,1)} fusion(bf16[256,64,32]{0,2,1:T(8,128)(2,1)} %all-gather.2.cloned.1.call-done, bf16[64]{0:T(256)(128)(2,1)S(1)} %get-tuple-element.45, bf16[256,8,32]{0,2,1:T(8,128)(2,1)S(1)} %copy.192), kind=kOutput, calls=%fused_computation.5 | convolution fusion | flops 271056896 | bytes 2228352 | tf_op jit(solution)/shard_map/while/body/eval_jaxpr/sic,sje->ijce/dot_general | solution.py:89
  121.7 7.7 %copy.193 = bf16[8,64,32,32]{1,3,2,0:T(8,128)(2,1)S(1)} copy(bf16[8,64,32,32]{2,3,0,1:T(8,128)(2,1)} %convert_bitcast_fusion) | data formatting | bytes 2097152 | tf_op jit(solution)/shard_map/while/body/eval_jaxpr/convert_element_type | solution.py:91
  129.4 0.8 fusion.80
  130.5 1.1 fusion.26
  (61 shorter events, 3.3 us)
Async XLA Ops:
  7.2 53.3 %copy-start = (bf16[1024,256]{1,0:T(8,128)(2,1)S(1)}, bf16[1024,256]{1,0:T(8,128)(2,1)}, u32[]{:S(2)}) copy-start(bf16[1024,256]{1,0:T(8,128)(2,1)} %param.27) | copy-start | bytes 1572868
  12.3 29.7 %copy-start.1 = (bf16[256,256]{1,0:T(8,128)(2,1)S(1)}, bf16[256,256]{1,0:T(8,128)(2,1)}, u32[]{:S(2)}) copy-start(bf16[256,256]{1,0:T(8,128)(2,1)} %param.21) | copy-start | bytes 393220
  18.5 23.9 %copy-start.2 = (bf16[256,256]{1,0:T(8,128)(2,1)S(1)}, bf16[256,256]{1,0:T(8,128)(2,1)}, u32[]{:S(2)}) copy-start(bf16[256,256]{1,0:T(8,128)(2,1)} %param.22) | copy-start | bytes 393220
  18.5 21.8 %all-to-all-start = ((bf16[16,16,1,4,256]{4,1,3,2,0:T(8,128)(2,1)}), bf16[16,16,1,4,256]{4,1,3,2,0:T(8,128)(2,1)S(1)}, u32[]{:S(2)}, u32[]{:S(2)}) async-start(bf16[16,16,1,4,256]{4,1,3,2,0:T(8,128)(2,1)} %constant_dynamic-update-slice_fusion), calls=%async_computation | async-start | bytes 1048576 | tf_op jit(solution)/shard_map/all_to_all | solution.py:150
  26.0 91.2 %all-gather.2.cloned.1.call-start = ((), (), s32[]{:S(2)}) async-start(), calls=%async_computation.4 | async-start | bytes 1114112 | tf_op jit(solution)/shard_map/all_gather | solution.py:166
  40.5 3.0 %copy-start.3 = (bf16[256,256]{1,0:T(8,128)(2,1)S(1)}, bf16[256,256]{1,0:T(8,128)(2,1)}, u32[]{:S(2)}) copy-start(bf16[256,256]{1,0:T(8,128)(2,1)} %param.23) | copy-start | bytes 393220
  50.9 6.9 %copy-start.6 = (bf16[256,256]{1,0:T(8,128)(2,1)S(1)}, bf16[256,256]{1,0:T(8,128)(2,1)}, u32[]{:S(2)}) copy-start(bf16[256,256]{1,0:T(8,128)(2,1)} %param.25) | copy-start | bytes 393220
  50.9 6.9 %copy-start.7 = (bf16[256,256]{1,0:T(8,128)(2,1)S(1)}, bf16[256,256]{1,0:T(8,128)(2,1)}, u32[]{:S(2)}) copy-start(bf16[256,256]{1,0:T(8,128)(2,1)} %param.24) | copy-start | bytes 393220
  59.2 4.1 %copy-start.11 = (bf16[256,32]{0,1:T(8,128)(2,1)S(1)}, bf16[256,32]{0,1:T(8,128)(2,1)}, u32[]{:S(2)}) copy-start(bf16[256,32]{0,1:T(8,128)(2,1)} %param.29) | copy-start | bytes 49156
  59.2 5.0 %copy-start.12 = (bf16[256,32]{0,1:T(8,128)(2,1)S(1)}, bf16[256,32]{0,1:T(8,128)(2,1)}, u32[]{:S(2)}) copy-start(bf16[256,32]{0,1:T(8,128)(2,1)} %param.28) | copy-start | bytes 49156
  63.1 38.9 %copy-start.4 = (s32[128]{0:T(128)S(1)}, s32[128]{0:T(128)}, u32[]{:S(2)}) copy-start(s32[128]{0:T(128)} %param.20) | copy-start | bytes 1540
  85.7 12.5 %all-to-all-start.3 = ((bf16[16,2,2048]{2,1,0:T(2,128)(2,1)}), bf16[16,2,2048]{2,1,0:T(2,128)(2,1)S(1)}, u32[]{:S(2)}, u32[]{:S(2)}) async-start(bf16[16,2,2048]{2,1,0:T(2,128)(2,1)} %reshape.148), calls=%async_computation.3 | async-start | bytes 262144 | tf_op jit(solution)/shard_map/all_to_all | solution.py:168
  98.3 17.8 %all-to-all-start.1 = ((bf16[256,4,256]{2,1,0:T(4,128)(2,1)}), bf16[256,4,256]{2,1,0:T(4,128)(2,1)S(1)}, u32[]{:S(2)}, u32[]{:S(2)}) async-start(bf16[256,4,256]{2,1,0:T(4,128)(2,1)} %copy.182), calls=%async_computation.1 | async-start | bytes 1048576 | tf_op jit(solution)/shard_map/all_to_all | solution.py:163
  121.6 7.7 %copy-start.5 = (bf16[1024,128]{1,0:T(8,128)(2,1)S(1)}, bf16[1024,128]{1,0:T(8,128)(2,1)}, u32[]{:S(2)}) copy-start(bf16[1024,128]{1,0:T(8,128)(2,1)} %param.30) | copy-start | bytes 786436
  121.6 7.7 %copy-start.8 = (bf16[8,64,128]{2,1,0:T(8,128)(2,1)S(1)}, bf16[8,64,128]{2,1,0:T(8,128)(2,1)}, u32[]{:S(2)}) copy-start(bf16[8,64,128]{2,1,0:T(8,128)(2,1)} %param.18) | copy-start | bytes 393220
  121.6 7.7 %copy-start.13 = (f32[128]{0:T(128)S(1)}, f32[128]{0:T(128)}, u32[]{:S(2)}) copy-start(f32[128]{0:T(128)} %param.31) | copy-start | bytes 1540
  121.6 8.9 %copy-start.9 = (bf16[512,128]{1,0:T(8,128)(2,1)S(1)}, bf16[512,128]{1,0:T(8,128)(2,1)}, u32[]{:S(2)}) copy-start(bf16[512,128]{1,0:T(8,128)(2,1)} %param.33) | copy-start | bytes 393220
  121.6 8.9 %copy-start.10 = (bf16[128,512]{1,0:T(8,128)(2,1)S(1)}, bf16[128,512]{1,0:T(8,128)(2,1)}, u32[]{:S(2)}) copy-start(bf16[128,512]{1,0:T(8,128)(2,1)} %param.32) | copy-start | bytes 393220
Sparse Core Ops, SparseCore 0:
  64.4 37.4 all-gather.1
